TPU v7x, 32 devices: a whole 2x2x4 slice. The times are simulated.
32 devices in a mesh: pop: 8 (over y, x, core), tile: 4 (over z).
Axes of the slice: x: 2, y: 2, z: 4, core: 2. Of those that a mesh axis runs over, the one named last changes fastest.
Arguments:
- weights: int32 [8, 8], replicated, may hold values from -2 to 3
- terminal: float32 [8, 32, 2048], P('pop', 'tile'), may hold values from -4.5 to 4.5
- density_history: bfloat16 [8, 8, 32, 2048], P('pop', None, 'tile'), may hold values from 0.19921875 to 2
- density_init: float32 [8, 32, 2048], P('pop', 'tile'), may hold values from 0.2 to 2
Outputs:
- values: float32 [8, 8, 32, 2048], P('pop', None, 'tile')
- density_final: float32 [8, 32, 2048], P('pop', 'tile')
All inputs are finite; a program needn't handle non-finite values.
Results may differ from a plain program's by a relative error of at most 0.0003.
Values may be sent and summed in bfloat16 or wider, within the bound.
A program may use at most 64 MiB of HBM per device.

v0:
```python
import jax
import jax.numpy as jnp
from jax import lax
from jax.sharding import PartitionSpec as P

time_step = 0.2
viscosity = 0.2


def padded_2(x, sides, width):
    for axis, dim in sides:
        peers, length = (lax.axis_size(axis), x.shape[dim])
        up = [(i, (i + 1) % peers) for i in range(peers)]
        down = [(j, i) for i, j in up]
        last = lax.slice_in_dim(x, length - width, length, axis=dim)
        leading = lax.slice_in_dim(x, 0, width, axis=dim)
        before = lax.ppermute(last, axis, up)
        after = lax.ppermute(leading, axis, down)
        x = jnp.concatenate([before, x, after], axis=dim)
    return x


def laplace_padded(padded):
    center = padded[:, 1:-1]
    return (
        padded[:, 2:]
        + padded[:, :-2]
        + jnp.roll(center, -1, 2)
        + jnp.roll(center, 1, 2)
        - 4.0 * center
    )


def hamiltonian_padded(padded):
    center = padded[:, 1:-1]
    ahead_rows = jnp.minimum(padded[:, 2:] - center, 0.0)
    behind_rows = jnp.maximum(center - padded[:, :-2], 0.0)
    ahead_cols = jnp.minimum(jnp.roll(center, -1, 2) - center, 0.0)
    behind_cols = jnp.maximum(center - jnp.roll(center, 1, 2), 0.0)
    return 0.5 * (
        behind_rows * behind_rows
        + ahead_rows * ahead_rows
        + behind_cols * behind_cols
        + ahead_cols * ahead_cols
    )


def transport_padded(padded_mass, padded_value):
    center = padded_mass[:, 1:-1]
    value_mid = padded_value[:, 1:-1]
    drift_rows = -(padded_value[:, 1:] - padded_value[:, :-1])
    flux_rows = (
        jnp.maximum(drift_rows, 0.0) * padded_mass[:, :-1]
        + jnp.minimum(drift_rows, 0.0) * padded_mass[:, 1:]
    )
    drift_cols = -(jnp.roll(value_mid, -1, 2) - value_mid)
    flux_cols = jnp.maximum(drift_cols, 0.0) * center + jnp.minimum(drift_cols, 0.0) * jnp.roll(
        center, -1, 2
    )
    div_rows = flux_rows[:, 1:] - flux_rows[:, :-1]
    div_cols = flux_cols - jnp.roll(flux_cols, 1, 2)
    return center + time_step * (viscosity * laplace_padded(padded_mass) - div_rows - div_cols)


def per_device(weights, terminal, density_history, density_init):
    populations = weights.shape[0]
    horizon = density_history.shape[1]
    own_index = lax.axis_index("pop")
    own_weights = lax.dynamic_slice_in_dim(weights, own_index, 1, 0)[0].astype(jnp.float32)
    total_cells = terminal.shape[1] * lax.axis_size("tile") * terminal.shape[2]
    coupled_all = (
        jnp.tensordot(
            own_weights,
            lax.all_gather(density_history, "pop", axis=0, tiled=True).astype(jnp.float32),
            axes=1,
            precision=lax.Precision.HIGHEST,
        )
        / populations
    )
    current = terminal
    kept_rims = [None] * horizon
    fields = [None] * horizon
    local_sums = [None] * horizon
    for step in reversed(range(horizon)):
        coupled = coupled_all[step][None]
        padded = padded_2(current, (("tile", 1),), 1)
        if step + 1 < horizon:
            kept_rims[step + 1] = padded
        advanced = current + time_step * (
            viscosity * laplace_padded(padded) - hamiltonian_padded(padded) + coupled
        )
        local_sums[step] = jnp.sum(advanced)
        fields[step] = advanced
        current = advanced
    grid_sums = lax.psum(jnp.stack(local_sums), "tile")
    centred = [fields[step] - grid_sums[step] / total_cells for step in range(horizon)]
    density = density_init
    for step in range(horizon):
        stacked = padded_2(jnp.concatenate([density, fields[step]], 0), (("tile", 1),), 1)
        padded_mass = stacked[:1]
        padded_value = stacked[1:]
        density = transport_padded(padded_mass, padded_value)
    return (jnp.stack(centred, axis=1), density)


def solution(mesh):
    in_specs = (P(), P("pop", "tile", None), P("pop", None, "tile", None), P("pop", "tile", None))
    out_specs = (P("pop", None, "tile", None), P("pop", "tile", None))
    return jax.shard_map(
        per_device, mesh=mesh, in_specs=in_specs, out_specs=out_specs, check_vma=False
    )
```

profile of v0, /device:TPU:0, one launch (start us, length us, event | category | flops | bytes accessed | tf_op | source)
XLA Modules:
  0.0 176.4 jit_solution(12679024923004292825)
XLA Ops:
  8.8 5.1 %collective-permute-start = (f32[1,1,2048]{2,1,0:T(1,128)S(1)}, f32[1,1,2048]{2,1,0:T(1,128)S(1)}, u32[]{:S(2)}, u32[]{:S(2)}) collective-permute-start(f32[1,1,2048]{2,1,0:T(1,128)S(1)} %get-tuple-element.124), channel_id=1, source_target_pairs={{1,0},{2,1},{3,2},{0,3},{5,4},{6,5},{7,6},{4,7},{9,8},{10,9},{11,1... | collective-permute-start | bytes 24584 | tf_op jit(solution)/shard_map/ppermute | solution.py:18
  17.5 22.9 %all-gather.2.cloned.1.call-done = bf16[8,8,8,2048]{3,2,1,0:T(8,128)(2,1)} async-done(((bf16[1,8,8,2048]{3,2,1,0:T(8,128)(2,1)}), bf16[8,8,8,2048]{3,2,1,0:T(8,128)(2,1)}) %all-gather.2.cloned.1.call-update) | async-done | bytes 2097168 | tf_op jit(solution)/shard_map/all_gather | solution.py:74
  40.4 4.3 %fusion = f32[1,8,8,2048]{3,0,2,1:T(1,128)S(1)} fusion(bf16[8,8,8,2048]{3,2,1,0:T(8,128)(2,1)} %all-gather.2.cloned.1.call-done, s32[8,8]{1,0:T(8,128)} %param.4, s32[]{:T(128)S(6)} %select_n.3), kind=kOutput, calls=%fused_computation | convolution fusion | flops 12582920 | bytes 2621956 | tf_op jit(solution)/shard_map/dot_general | solution.py:72
  47.4 3.4 %collective-permute-start.2 = (f32[1,1,2048]{2,1,0:T(1,128)S(1)}, f32[1,1,2048]{2,1,0:T(1,128)S(1)}, u32[]{:S(2)}, u32[]{:S(2)}) collective-permute-start(f32[1,1,2048]{2,1,0:T(1,128)S(1)} %get-tuple-element.118), channel_id=1, source_target_pairs={{1,0},{2,1},{3,2},{0,3},{5,4},{6,5},{7,6},{4,7},{9,8},{10,9},{11,1... | collective-permute-start | bytes 24584 | tf_op jit(solution)/shard_map/ppermute | solution.py:18
  52.1 4.1 %collective-permute-done.3 = f32[1,1,2048]{2,1,0:T(1,128)S(1)} collective-permute-done((f32[1,1,2048]{2,1,0:T(1,128)S(1)}, f32[1,1,2048]{2,1,0:T(1,128)S(1)}, u32[]{:S(2)}, u32[]{:S(2)}) %collective-permute-start.3) | collective-permute-done | bytes 8224 | tf_op jit(solution)/shard_map/ppermute | solution.py:17
  56.2 1.6 fusion.240
  57.9 2.0 %collective-permute-start.5 = (f32[1,1,2048]{2,1,0:T(1,128)S(1)}, f32[1,1,2048]{2,1,0:T(1,128)S(1)}, u32[]{:S(2)}, u32[]{:S(2)}) collective-permute-start(f32[1,1,2048]{2,1,0:T(1,128)S(1)} %get-tuple-element.113), channel_id=1, source_target_pairs={{0,1},{1,2},{2,3},{3,0},{4,5},{5,6},{6,7},{7,4},{8,9},{9,10},{10,1... | collective-permute-start | bytes 24584 | tf_op jit(solution)/shard_map/ppermute | solution.py:17
  61.6 1.9 %collective-permute-done.5 = f32[1,1,2048]{2,1,0:T(1,128)S(1)} collective-permute-done((f32[1,1,2048]{2,1,0:T(1,128)S(1)}, f32[1,1,2048]{2,1,0:T(1,128)S(1)}, u32[]{:S(2)}, u32[]{:S(2)}) %collective-permute-start.5) | collective-permute-done | bytes 8224 | tf_op jit(solution)/shard_map/ppermute | solution.py:17
  65.1 2.0 %collective-permute-start.7 = (f32[1,1,2048]{2,1,0:T(1,128)S(1)}, f32[1,1,2048]{2,1,0:T(1,128)S(1)}, u32[]{:S(2)}, u32[]{:S(2)}) collective-permute-start(f32[1,1,2048]{2,1,0:T(1,128)S(1)} %get-tuple-element.107), channel_id=1, source_target_pairs={{0,1},{1,2},{2,3},{3,0},{4,5},{5,6},{6,7},{7,4},{8,9},{9,10},{10,1... | collective-permute-start | bytes 24584 | tf_op jit(solution)/shard_map/ppermute | solution.py:17
  68.7 1.9 %collective-permute-done.7 = f32[1,1,2048]{2,1,0:T(1,128)S(1)} collective-permute-done((f32[1,1,2048]{2,1,0:T(1,128)S(1)}, f32[1,1,2048]{2,1,0:T(1,128)S(1)}, u32[]{:S(2)}, u32[]{:S(2)}) %collective-permute-start.7) | collective-permute-done | bytes 8224 | tf_op jit(solution)/shard_map/ppermute | solution.py:17
  70.7 1.6 fusion.244
  72.4 2.0 %collective-permute-start.9 = (f32[1,1,2048]{2,1,0:T(1,128)S(1)}, f32[1,1,2048]{2,1,0:T(1,128)S(1)}, u32[]{:S(2)}, u32[]{:S(2)}) collective-permute-start(f32[1,1,2048]{2,1,0:T(1,128)S(1)} %get-tuple-element.101), channel_id=1, source_target_pairs={{0,1},{1,2},{2,3},{3,0},{4,5},{5,6},{6,7},{7,4},{8,9},{9,10},{10,1... | collective-permute-start | bytes 24584 | tf_op jit(solution)/shard_map/ppermute | solution.py:17
  76.1 1.9 %collective-permute-done.9 = f32[1,1,2048]{2,1,0:T(1,128)S(1)} collective-permute-done((f32[1,1,2048]{2,1,0:T(1,128)S(1)}, f32[1,1,2048]{2,1,0:T(1,128)S(1)}, u32[]{:S(2)}, u32[]{:S(2)}) %collective-permute-start.9) | collective-permute-done | bytes 8224 | tf_op jit(solution)/shard_map/ppermute | solution.py:17
  79.7 2.0 %collective-permute-start.11 = (f32[1,1,2048]{2,1,0:T(1,128)S(1)}, f32[1,1,2048]{2,1,0:T(1,128)S(1)}, u32[]{:S(2)}, u32[]{:S(2)}) collective-permute-start(f32[1,1,2048]{2,1,0:T(1,128)S(1)} %get-tuple-element.95), channel_id=1, source_target_pairs={{0,1},{1,2},{2,3},{3,0},{4,5},{5,6},{6,7},{7,4},{8,9},{9,10},{10,1... | collective-permute-start | bytes 24584 | tf_op jit(solution)/shard_map/ppermute | solution.py:17
  83.3 1.9 %collective-permute-done.11 = f32[1,1,2048]{2,1,0:T(1,128)S(1)} collective-permute-done((f32[1,1,2048]{2,1,0:T(1,128)S(1)}, f32[1,1,2048]{2,1,0:T(1,128)S(1)}, u32[]{:S(2)}, u32[]{:S(2)}) %collective-permute-start.11) | collective-permute-done | bytes 8224 | tf_op jit(solution)/shard_map/ppermute | solution.py:17
  86.9 2.0 %collective-permute-start.13 = (f32[1,1,2048]{2,1,0:T(1,128)S(1)}, f32[1,1,2048]{2,1,0:T(1,128)S(1)}, u32[]{:S(2)}, u32[]{:S(2)}) collective-permute-start(f32[1,1,2048]{2,1,0:T(1,128)S(1)} %get-tuple-element.89), channel_id=1, source_target_pairs={{0,1},{1,2},{2,3},{3,0},{4,5},{5,6},{6,7},{7,4},{8,9},{9,10},{10,1... | collective-permute-start | bytes 24584 | tf_op jit(solution)/shard_map/ppermute | solution.py:17
  90.5 1.9 %collective-permute-done.13 = f32[1,1,2048]{2,1,0:T(1,128)S(1)} collective-permute-done((f32[1,1,2048]{2,1,0:T(1,128)S(1)}, f32[1,1,2048]{2,1,0:T(1,128)S(1)}, u32[]{:S(2)}, u32[]{:S(2)}) %collective-permute-start.13) | collective-permute-done | bytes 8224 | tf_op jit(solution)/shard_map/ppermute | solution.py:17
  92.4 1.6 fusion.250
  94.1 2.0 %collective-permute-start.15 = (f32[1,1,2048]{2,1,0:T(1,128)S(1)}, f32[1,1,2048]{2,1,0:T(1,128)S(1)}, u32[]{:S(2)}, u32[]{:S(2)}) collective-permute-start(f32[1,1,2048]{2,1,0:T(1,128)S(1)} %get-tuple-element.83), channel_id=1, source_target_pairs={{0,1},{1,2},{2,3},{3,0},{4,5},{5,6},{6,7},{7,4},{8,9},{9,10},{10,1... | collective-permute-start | bytes 24584 | tf_op jit(solution)/shard_map/ppermute | solution.py:17
  97.8 1.9 %collective-permute-done.15 = f32[1,1,2048]{2,1,0:T(1,128)S(1)} collective-permute-done((f32[1,1,2048]{2,1,0:T(1,128)S(1)}, f32[1,1,2048]{2,1,0:T(1,128)S(1)}, u32[]{:S(2)}, u32[]{:S(2)}) %collective-permute-start.15) | collective-permute-done | bytes 8224 | tf_op jit(solution)/shard_map/ppermute | solution.py:17
  101.2 5.2 %stack.62 = f32[8]{0:T(128)S(1)} concatenate(f32[1]{0:T(128)} %bitcast.4, f32[1]{0:T(128)} %bitcast.5, f32[1]{0:T(128)} %bitcast.6, f32[1]{0:T(128)} %bitcast.7, f32[1]{0:T(128)} %bitcast.8, f32[1]{0:T(128)} %bitcast.9, f32[1]{0:T(128)} %bitcast.10, f32[1]{0:T(128)} %bitcast.11), dimensions={0} | concatenate | bytes 64 | tf_op jit(solution)/shard_map/stack | solution.py:95
  106.5 8.6 %psum.7 = f32[8]{0:T(128)S(1)} all-reduce(f32[8]{0:T(128)S(1)} %stack.62), channel_id=1, replica_groups=mesh['pop'=8,'tile'=4] {'tile'}, use_global_device_ids=true, to_apply=%region_8.9 | all-reduce | flops 8 | bytes 64 | tf_op jit(solution)/shard_map/psum | solution.py:95
  120.9 1.8 collective-permute-start.17
  122.7 2.1 %collective-permute-start.16 = (f32[2,1,2048]{2,1,0:T(1,128)S(1)}, f32[2,1,2048]{2,1,0:T(1,128)S(1)}, u32[]{:S(2)}, u32[]{:S(2)}) collective-permute-start(f32[2,1,2048]{2,1,0:T(1,128)S(1)} %get-tuple-element.49), channel_id=1, source_target_pairs={{1,0},{2,1},{3,2},{0,3},{5,4},{6,5},{7,6},{4,7},{9,8},{10,9},{11,1... | collective-permute-start | bytes 49160 | tf_op jit(solution)/shard_map/ppermute | solution.py:18
  127.1 3.8 %collective-permute-start.18 = (f32[2,1,2048]{2,1,0:T(1,128)S(1)}, f32[2,1,2048]{2,1,0:T(1,128)S(1)}, u32[]{:S(2)}, u32[]{:S(2)}) collective-permute-start(f32[2,1,2048]{2,1,0:T(1,128)S(1)} %get-tuple-element.45), channel_id=1, source_target_pairs={{1,0},{2,1},{3,2},{0,3},{5,4},{6,5},{7,6},{4,7},{9,8},{10,9},{11,1... | collective-permute-start | bytes 49160 | tf_op jit(solution)/shard_map/ppermute | solution.py:18
  134.0 2.9 %collective-permute-start.20 = (f32[2,1,2048]{2,1,0:T(1,128)S(1)}, f32[2,1,2048]{2,1,0:T(1,128)S(1)}, u32[]{:S(2)}, u32[]{:S(2)}) collective-permute-start(f32[2,1,2048]{2,1,0:T(1,128)S(1)} %get-tuple-element.41), channel_id=1, source_target_pairs={{1,0},{2,1},{3,2},{0,3},{5,4},{6,5},{7,6},{4,7},{9,8},{10,9},{11,1... | collective-permute-start | bytes 49160 | tf_op jit(solution)/shard_map/ppermute | solution.py:18
  140.2 2.8 %collective-permute-start.22 = (f32[2,1,2048]{2,1,0:T(1,128)S(1)}, f32[2,1,2048]{2,1,0:T(1,128)S(1)}, u32[]{:S(2)}, u32[]{:S(2)}) collective-permute-start(f32[2,1,2048]{2,1,0:T(1,128)S(1)} %get-tuple-element.37), channel_id=1, source_target_pairs={{1,0},{2,1},{3,2},{0,3},{5,4},{6,5},{7,6},{4,7},{9,8},{10,9},{11,1... | collective-permute-start | bytes 49160 | tf_op jit(solution)/shard_map/ppermute | solution.py:18
  143.1 1.6 collective-permute-done.23
  146.3 2.7 %collective-permute-start.24 = (f32[2,1,2048]{2,1,0:T(1,128)S(1)}, f32[2,1,2048]{2,1,0:T(1,128)S(1)}, u32[]{:S(2)}, u32[]{:S(2)}) collective-permute-start(f32[2,1,2048]{2,1,0:T(1,128)S(1)} %get-tuple-element.33), channel_id=1, source_target_pairs={{1,0},{2,1},{3,2},{0,3},{5,4},{6,5},{7,6},{4,7},{9,8},{10,9},{11,1... | collective-permute-start | bytes 49160 | tf_op jit(solution)/shard_map/ppermute | solution.py:18
  152.4 2.7 %collective-permute-start.26 = (f32[2,1,2048]{2,1,0:T(1,128)S(1)}, f32[2,1,2048]{2,1,0:T(1,128)S(1)}, u32[]{:S(2)}, u32[]{:S(2)}) collective-permute-start(f32[2,1,2048]{2,1,0:T(1,128)S(1)} %get-tuple-element.29), channel_id=1, source_target_pairs={{1,0},{2,1},{3,2},{0,3},{5,4},{6,5},{7,6},{4,7},{9,8},{10,9},{11,1... | collective-permute-start | bytes 49160 | tf_op jit(solution)/shard_map/ppermute | solution.py:18
  158.4 2.7 %collective-permute-start.28 = (f32[2,1,2048]{2,1,0:T(1,128)S(1)}, f32[2,1,2048]{2,1,0:T(1,128)S(1)}, u32[]{:S(2)}, u32[]{:S(2)}) collective-permute-start(f32[2,1,2048]{2,1,0:T(1,128)S(1)} %get-tuple-element.25), channel_id=1, source_target_pairs={{1,0},{2,1},{3,2},{0,3},{5,4},{6,5},{7,6},{4,7},{9,8},{10,9},{11,1... | collective-permute-start | bytes 49160 | tf_op jit(solution)/shard_map/ppermute | solution.py:18
  164.4 2.7 %collective-permute-start.30 = (f32[2,1,2048]{2,1,0:T(1,128)S(1)}, f32[2,1,2048]{2,1,0:T(1,128)S(1)}, u32[]{:S(2)}, u32[]{:S(2)}) collective-permute-start(f32[2,1,2048]{2,1,0:T(1,128)S(1)} %get-tuple-element.21), channel_id=1, source_target_pairs={{1,0},{2,1},{3,2},{0,3},{5,4},{6,5},{7,6},{4,7},{9,8},{10,9},{11,1... | collective-permute-start | bytes 49160 | tf_op jit(solution)/shard_map/ppermute | solution.py:18
  (152 shorter events, 49.5 us)
Async XLA Ops:
  7.2 33.2 %all-gather.2.cloned.1.call-start = ((), (), s32[]{:S(2)}) async-start(), calls=%async_computation | async-start | bytes 2359296 | tf_op jit(solution)/shard_map/all_gather | solution.py:74
  8.8 36.9 %collective-permute-start = (f32[1,1,2048]{2,1,0:T(1,128)S(1)}, f32[1,1,2048]{2,1,0:T(1,128)S(1)}, u32[]{:S(2)}, u32[]{:S(2)}) collective-permute-start(f32[1,1,2048]{2,1,0:T(1,128)S(1)} %get-tuple-element.124), channel_id=1, source_target_pairs={{1,0},{2,1},{3,2},{0,3},{5,4},{6,5},{7,6},{4,7},{9,8},{10,9},{11,1... | collective-permute-start | bytes 24584 | tf_op jit(solution)/shard_map/ppermute | solution.py:18
  14.0 31.7 %collective-permute-start.1 = (f32[1,1,2048]{2,1,0:T(1,128)S(1)}, f32[1,1,2048]{2,1,0:T(1,128)S(1)}, u32[]{:S(2)}, u32[]{:S(2)}) collective-permute-start(f32[1,1,2048]{2,1,0:T(1,128)S(1)} %get-tuple-element.125), channel_id=1, source_target_pairs={{0,1},{1,2},{2,3},{3,0},{4,5},{5,6},{6,7},{7,4},{8,9},{9,10},{10,1... | collective-permute-start | bytes 24584 | tf_op jit(solution)/shard_map/ppermute | solution.py:17
  47.4 4.7 %collective-permute-start.2 = (f32[1,1,2048]{2,1,0:T(1,128)S(1)}, f32[1,1,2048]{2,1,0:T(1,128)S(1)}, u32[]{:S(2)}, u32[]{:S(2)}) collective-permute-start(f32[1,1,2048]{2,1,0:T(1,128)S(1)} %get-tuple-element.118), channel_id=1, source_target_pairs={{1,0},{2,1},{3,2},{0,3},{5,4},{6,5},{7,6},{4,7},{9,8},{10,9},{11,1... | collective-permute-start | bytes 24584 | tf_op jit(solution)/shard_map/ppermute | solution.py:18
  50.7 5.4 %collective-permute-start.3 = (f32[1,1,2048]{2,1,0:T(1,128)S(1)}, f32[1,1,2048]{2,1,0:T(1,128)S(1)}, u32[]{:S(2)}, u32[]{:S(2)}) collective-permute-start(f32[1,1,2048]{2,1,0:T(1,128)S(1)} %get-tuple-element.119), channel_id=1, source_target_pairs={{0,1},{1,2},{2,3},{3,0},{4,5},{5,6},{6,7},{7,4},{8,9},{9,10},{10,1... | collective-permute-start | bytes 24584 | tf_op jit(solution)/shard_map/ppermute | solution.py:17
  57.9 3.7 %collective-permute-start.4 = (f32[1,1,2048]{2,1,0:T(1,128)S(1)}, f32[1,1,2048]{2,1,0:T(1,128)S(1)}, u32[]{:S(2)}, u32[]{:S(2)}) collective-permute-start(f32[1,1,2048]{2,1,0:T(1,128)S(1)} %get-tuple-element.112), channel_id=1, source_target_pairs={{1,0},{2,1},{3,2},{0,3},{5,4},{6,5},{7,6},{4,7},{9,8},{10,9},{11,1... | collective-permute-start | bytes 24584 | tf_op jit(solution)/shard_map/ppermute | solution.py:18
  57.9 5.5 %collective-permute-start.5 = (f32[1,1,2048]{2,1,0:T(1,128)S(1)}, f32[1,1,2048]{2,1,0:T(1,128)S(1)}, u32[]{:S(2)}, u32[]{:S(2)}) collective-permute-start(f32[1,1,2048]{2,1,0:T(1,128)S(1)} %get-tuple-element.113), channel_id=1, source_target_pairs={{0,1},{1,2},{2,3},{3,0},{4,5},{5,6},{6,7},{7,4},{8,9},{9,10},{10,1... | collective-permute-start | bytes 24584 | tf_op jit(solution)/shard_map/ppermute | solution.py:17
  65.1 3.7 %collective-permute-start.6 = (f32[1,1,2048]{2,1,0:T(1,128)S(1)}, f32[1,1,2048]{2,1,0:T(1,128)S(1)}, u32[]{:S(2)}, u32[]{:S(2)}) collective-permute-start(f32[1,1,2048]{2,1,0:T(1,128)S(1)} %get-tuple-element.106), channel_id=1, source_target_pairs={{1,0},{2,1},{3,2},{0,3},{5,4},{6,5},{7,6},{4,7},{9,8},{10,9},{11,1... | collective-permute-start | bytes 24584 | tf_op jit(solution)/shard_map/ppermute | solution.py:18
  65.1 5.6 %collective-permute-start.7 = (f32[1,1,2048]{2,1,0:T(1,128)S(1)}, f32[1,1,2048]{2,1,0:T(1,128)S(1)}, u32[]{:S(2)}, u32[]{:S(2)}) collective-permute-start(f32[1,1,2048]{2,1,0:T(1,128)S(1)} %get-tuple-element.107), channel_id=1, source_target_pairs={{0,1},{1,2},{2,3},{3,0},{4,5},{5,6},{6,7},{7,4},{8,9},{9,10},{10,1... | collective-permute-start | bytes 24584 | tf_op jit(solution)/shard_map/ppermute | solution.py:17
  72.4 3.7 %collective-permute-start.8 = (f32[1,1,2048]{2,1,0:T(1,128)S(1)}, f32[1,1,2048]{2,1,0:T(1,128)S(1)}, u32[]{:S(2)}, u32[]{:S(2)}) collective-permute-start(f32[1,1,2048]{2,1,0:T(1,128)S(1)} %get-tuple-element.100), channel_id=1, source_target_pairs={{1,0},{2,1},{3,2},{0,3},{5,4},{6,5},{7,6},{4,7},{9,8},{10,9},{11,1... | collective-permute-start | bytes 24584 | tf_op jit(solution)/shard_map/ppermute | solution.py:18
  72.4 5.5 %collective-permute-start.9 = (f32[1,1,2048]{2,1,0:T(1,128)S(1)}, f32[1,1,2048]{2,1,0:T(1,128)S(1)}, u32[]{:S(2)}, u32[]{:S(2)}) collective-permute-start(f32[1,1,2048]{2,1,0:T(1,128)S(1)} %get-tuple-element.101), channel_id=1, source_target_pairs={{0,1},{1,2},{2,3},{3,0},{4,5},{5,6},{6,7},{7,4},{8,9},{9,10},{10,1... | collective-permute-start | bytes 24584 | tf_op jit(solution)/shard_map/ppermute | solution.py:17
  79.6 3.7 %collective-permute-start.10 = (f32[1,1,2048]{2,1,0:T(1,128)S(1)}, f32[1,1,2048]{2,1,0:T(1,128)S(1)}, u32[]{:S(2)}, u32[]{:S(2)}) collective-permute-start(f32[1,1,2048]{2,1,0:T(1,128)S(1)} %get-tuple-element.94), channel_id=1, source_target_pairs={{1,0},{2,1},{3,2},{0,3},{5,4},{6,5},{7,6},{4,7},{9,8},{10,9},{11,1... | collective-permute-start | bytes 24584 | tf_op jit(solution)/shard_map/ppermute | solution.py:18
  79.7 5.5 %collective-permute-start.11 = (f32[1,1,2048]{2,1,0:T(1,128)S(1)}, f32[1,1,2048]{2,1,0:T(1,128)S(1)}, u32[]{:S(2)}, u32[]{:S(2)}) collective-permute-start(f32[1,1,2048]{2,1,0:T(1,128)S(1)} %get-tuple-element.95), channel_id=1, source_target_pairs={{0,1},{1,2},{2,3},{3,0},{4,5},{5,6},{6,7},{7,4},{8,9},{9,10},{10,1... | collective-permute-start | bytes 24584 | tf_op jit(solution)/shard_map/ppermute | solution.py:17
  86.8 3.7 %collective-permute-start.12 = (f32[1,1,2048]{2,1,0:T(1,128)S(1)}, f32[1,1,2048]{2,1,0:T(1,128)S(1)}, u32[]{:S(2)}, u32[]{:S(2)}) collective-permute-start(f32[1,1,2048]{2,1,0:T(1,128)S(1)} %get-tuple-element.88), channel_id=1, source_target_pairs={{1,0},{2,1},{3,2},{0,3},{5,4},{6,5},{7,6},{4,7},{9,8},{10,9},{11,1... | collective-permute-start | bytes 24584 | tf_op jit(solution)/shard_map/ppermute | solution.py:18
  86.9 5.5 %collective-permute-start.13 = (f32[1,1,2048]{2,1,0:T(1,128)S(1)}, f32[1,1,2048]{2,1,0:T(1,128)S(1)}, u32[]{:S(2)}, u32[]{:S(2)}) collective-permute-start(f32[1,1,2048]{2,1,0:T(1,128)S(1)} %get-tuple-element.89), channel_id=1, source_target_pairs={{0,1},{1,2},{2,3},{3,0},{4,5},{5,6},{6,7},{7,4},{8,9},{9,10},{10,1... | collective-permute-start | bytes 24584 | tf_op jit(solution)/shard_map/ppermute | solution.py:17
  94.1 5.5 %collective-permute-start.15 = (f32[1,1,2048]{2,1,0:T(1,128)S(1)}, f32[1,1,2048]{2,1,0:T(1,128)S(1)}, u32[]{:S(2)}, u32[]{:S(2)}) collective-permute-start(f32[1,1,2048]{2,1,0:T(1,128)S(1)} %get-tuple-element.83), channel_id=1, source_target_pairs={{0,1},{1,2},{2,3},{3,0},{4,5},{5,6},{6,7},{7,4},{8,9},{9,10},{10,1... | collective-permute-start | bytes 24584 | tf_op jit(solution)/shard_map/ppermute | solution.py:17
  120.9 5.7 %collective-permute-start.17 = (f32[2,1,2048]{2,1,0:T(1,128)S(1)}, f32[2,1,2048]{2,1,0:T(1,128)S(1)}, u32[]{:S(2)}, u32[]{:S(2)}) collective-permute-start(f32[2,1,2048]{2,1,0:T(1,128)S(1)} %get-tuple-element.48), channel_id=1, source_target_pairs={{0,1},{1,2},{2,3},{3,0},{4,5},{5,6},{6,7},{7,4},{8,9},{9,10},{10,1... | collective-permute-start | bytes 49160 | tf_op jit(solution)/shard_map/ppermute | solution.py:17
  122.7 4.0 %collective-permute-start.16 = (f32[2,1,2048]{2,1,0:T(1,128)S(1)}, f32[2,1,2048]{2,1,0:T(1,128)S(1)}, u32[]{:S(2)}, u32[]{:S(2)}) collective-permute-start(f32[2,1,2048]{2,1,0:T(1,128)S(1)} %get-tuple-element.49), channel_id=1, source_target_pairs={{1,0},{2,1},{3,2},{0,3},{5,4},{6,5},{7,6},{4,7},{9,8},{10,9},{11,1... | collective-permute-start | bytes 49160 | tf_op jit(solution)/shard_map/ppermute | solution.py:18
  127.1 5.6 %collective-permute-start.19 = (f32[2,1,2048]{2,1,0:T(1,128)S(1)}, f32[2,1,2048]{2,1,0:T(1,128)S(1)}, u32[]{:S(2)}, u32[]{:S(2)}) collective-permute-start(f32[2,1,2048]{2,1,0:T(1,128)S(1)} %get-tuple-element.44), channel_id=1, source_target_pairs={{0,1},{1,2},{2,3},{3,0},{4,5},{5,6},{6,7},{7,4},{8,9},{9,10},{10,1... | collective-permute-start | bytes 49160 | tf_op jit(solution)/shard_map/ppermute | solution.py:17
  127.1 5.5 %collective-permute-start.18 = (f32[2,1,2048]{2,1,0:T(1,128)S(1)}, f32[2,1,2048]{2,1,0:T(1,128)S(1)}, u32[]{:S(2)}, u32[]{:S(2)}) collective-permute-start(f32[2,1,2048]{2,1,0:T(1,128)S(1)} %get-tuple-element.45), channel_id=1, source_target_pairs={{1,0},{2,1},{3,2},{0,3},{5,4},{6,5},{7,6},{4,7},{9,8},{10,9},{11,1... | collective-permute-start | bytes 49160 | tf_op jit(solution)/shard_map/ppermute | solution.py:18
  133.0 5.6 %collective-permute-start.21 = (f32[2,1,2048]{2,1,0:T(1,128)S(1)}, f32[2,1,2048]{2,1,0:T(1,128)S(1)}, u32[]{:S(2)}, u32[]{:S(2)}) collective-permute-start(f32[2,1,2048]{2,1,0:T(1,128)S(1)} %get-tuple-element.40), channel_id=1, source_target_pairs={{0,1},{1,2},{2,3},{3,0},{4,5},{5,6},{6,7},{7,4},{8,9},{9,10},{10,1... | collective-permute-start | bytes 49160 | tf_op jit(solution)/shard_map/ppermute | solution.py:17
  134.0 4.6 %collective-permute-start.20 = (f32[2,1,2048]{2,1,0:T(1,128)S(1)}, f32[2,1,2048]{2,1,0:T(1,128)S(1)}, u32[]{:S(2)}, u32[]{:S(2)}) collective-permute-start(f32[2,1,2048]{2,1,0:T(1,128)S(1)} %get-tuple-element.41), channel_id=1, source_target_pairs={{1,0},{2,1},{3,2},{0,3},{5,4},{6,5},{7,6},{4,7},{9,8},{10,9},{11,1... | collective-permute-start | bytes 49160 | tf_op jit(solution)/shard_map/ppermute | solution.py:18
  139.0 5.7 %collective-permute-start.23 = (f32[2,1,2048]{2,1,0:T(1,128)S(1)}, f32[2,1,2048]{2,1,0:T(1,128)S(1)}, u32[]{:S(2)}, u32[]{:S(2)}) collective-permute-start(f32[2,1,2048]{2,1,0:T(1,128)S(1)} %get-tuple-element.36), channel_id=1, source_target_pairs={{0,1},{1,2},{2,3},{3,0},{4,5},{5,6},{6,7},{7,4},{8,9},{9,10},{10,1... | collective-permute-start | bytes 49160 | tf_op jit(solution)/shard_map/ppermute | solution.py:17
  140.2 4.5 %collective-permute-start.22 = (f32[2,1,2048]{2,1,0:T(1,128)S(1)}, f32[2,1,2048]{2,1,0:T(1,128)S(1)}, u32[]{:S(2)}, u32[]{:S(2)}) collective-permute-start(f32[2,1,2048]{2,1,0:T(1,128)S(1)} %get-tuple-element.37), channel_id=1, source_target_pairs={{1,0},{2,1},{3,2},{0,3},{5,4},{6,5},{7,6},{4,7},{9,8},{10,9},{11,1... | collective-permute-start | bytes 49160 | tf_op jit(solution)/shard_map/ppermute | solution.py:18
  145.1 5.6 %collective-permute-start.25 = (f32[2,1,2048]{2,1,0:T(1,128)S(1)}, f32[2,1,2048]{2,1,0:T(1,128)S(1)}, u32[]{:S(2)}, u32[]{:S(2)}) collective-permute-start(f32[2,1,2048]{2,1,0:T(1,128)S(1)} %get-tuple-element.32), channel_id=1, source_target_pairs={{0,1},{1,2},{2,3},{3,0},{4,5},{5,6},{6,7},{7,4},{8,9},{9,10},{10,1... | collective-permute-start | bytes 49160 | tf_op jit(solution)/shard_map/ppermute | solution.py:17
  146.3 4.4 %collective-permute-start.24 = (f32[2,1,2048]{2,1,0:T(1,128)S(1)}, f32[2,1,2048]{2,1,0:T(1,128)S(1)}, u32[]{:S(2)}, u32[]{:S(2)}) collective-permute-start(f32[2,1,2048]{2,1,0:T(1,128)S(1)} %get-tuple-element.33), channel_id=1, source_target_pairs={{1,0},{2,1},{3,2},{0,3},{5,4},{6,5},{7,6},{4,7},{9,8},{10,9},{11,1... | collective-permute-start | bytes 49160 | tf_op jit(solution)/shard_map/ppermute | solution.py:18
  151.1 5.6 %collective-permute-start.27 = (f32[2,1,2048]{2,1,0:T(1,128)S(1)}, f32[2,1,2048]{2,1,0:T(1,128)S(1)}, u32[]{:S(2)}, u32[]{:S(2)}) collective-permute-start(f32[2,1,2048]{2,1,0:T(1,128)S(1)} %get-tuple-element.28), channel_id=1, source_target_pairs={{0,1},{1,2},{2,3},{3,0},{4,5},{5,6},{6,7},{7,4},{8,9},{9,10},{10,1... | collective-permute-start | bytes 49160 | tf_op jit(solution)/shard_map/ppermute | solution.py:17
  152.4 4.3 %collective-permute-start.26 = (f32[2,1,2048]{2,1,0:T(1,128)S(1)}, f32[2,1,2048]{2,1,0:T(1,128)S(1)}, u32[]{:S(2)}, u32[]{:S(2)}) collective-permute-start(f32[2,1,2048]{2,1,0:T(1,128)S(1)} %get-tuple-element.29), channel_id=1, source_target_pairs={{1,0},{2,1},{3,2},{0,3},{5,4},{6,5},{7,6},{4,7},{9,8},{10,9},{11,1... | collective-permute-start | bytes 49160 | tf_op jit(solution)/shard_map/ppermute | solution.py:18
  157.1 5.6 %collective-permute-start.29 = (f32[2,1,2048]{2,1,0:T(1,128)S(1)}, f32[2,1,2048]{2,1,0:T(1,128)S(1)}, u32[]{:S(2)}, u32[]{:S(2)}) collective-permute-start(f32[2,1,2048]{2,1,0:T(1,128)S(1)} %get-tuple-element.24), channel_id=1, source_target_pairs={{0,1},{1,2},{2,3},{3,0},{4,5},{5,6},{6,7},{7,4},{8,9},{9,10},{10,1... | collective-permute-start | bytes 49160 | tf_op jit(solution)/shard_map/ppermute | solution.py:17
  158.4 4.3 %collective-permute-start.28 = (f32[2,1,2048]{2,1,0:T(1,128)S(1)}, f32[2,1,2048]{2,1,0:T(1,128)S(1)}, u32[]{:S(2)}, u32[]{:S(2)}) collective-permute-start(f32[2,1,2048]{2,1,0:T(1,128)S(1)} %get-tuple-element.25), channel_id=1, source_target_pairs={{1,0},{2,1},{3,2},{0,3},{5,4},{6,5},{7,6},{4,7},{9,8},{10,9},{11,1... | collective-permute-start | bytes 49160 | tf_op jit(solution)/shard_map/ppermute | solution.py:18
  163.1 5.6 %collective-permute-start.31 = (f32[2,1,2048]{2,1,0:T(1,128)S(1)}, f32[2,1,2048]{2,1,0:T(1,128)S(1)}, u32[]{:S(2)}, u32[]{:S(2)}) collective-permute-start(f32[2,1,2048]{2,1,0:T(1,128)S(1)} %get-tuple-element.20), channel_id=1, source_target_pairs={{0,1},{1,2},{2,3},{3,0},{4,5},{5,6},{6,7},{7,4},{8,9},{9,10},{10,1... | collective-permute-start | bytes 49160 | tf_op jit(solution)/shard_map/ppermute | solution.py:17
  164.4 4.3 %collective-permute-start.30 = (f32[2,1,2048]{2,1,0:T(1,128)S(1)}, f32[2,1,2048]{2,1,0:T(1,128)S(1)}, u32[]{:S(2)}, u32[]{:S(2)}) collective-permute-start(f32[2,1,2048]{2,1,0:T(1,128)S(1)} %get-tuple-element.21), channel_id=1, source_target_pairs={{1,0},{2,1},{3,2},{0,3},{5,4},{6,5},{7,6},{4,7},{9,8},{10,9},{11,1... | collective-permute-start | bytes 49160 | tf_op jit(solution)/shard_map/ppermute | solution.py:18
  (4 other events, 85.1 us)
Sparse Core Ops, SparseCore 0:
  9.9 30.4 all-gather.1
where the time goes:
time: 177 us; the launch traced here: 176 us
  waiting for transfers between devices  61.8 us (35%)
  starting transfers between devices  52.1 us (29%)
  between operations  19.6 us (11%)
  other arithmetic  16.8 us (9%)
  local copies, waits for them, and re-layouts  13.3 us (8%)
  blocking collectives  8.62 us (5%)
  matrix products  4.31 us (2%)
    ppermute x16, starting transfers between devices, padded_2(): after = lax.ppermute(leading, axis, down)  30.9 us
    ppermute x16, waiting for transfers between devices, padded_2(): before = lax.ppermute(last, axis, up)  27.6 us
    all_gather x1, waiting for transfers between devices, per_device(): lax.all_gather(density_history, 'pop', axis=0, tiled=True)  22.9 us
    ppermute x16, starting transfers between devices, padded_2(): before = lax.ppermute(last, axis, up)  21.1 us
    reduce_sum x8, other arithmetic, per_device(): local_sums[step] = jnp.sum(advanced)  12.7 us
    ppermute x16, waiting for transfers between devices, padded_2(): after = lax.ppermute(leading, axis, down)  10.6 us
    psum x1, blocking collectives, per_device(): grid_sums = lax.psum(jnp.stack(local_sums), 'tile')  8.62 us
    slice x32, local copies, waits for them, and re-layouts, laplace_padded(): jnp.roll(center, -1, 2)  5.71 us
  transfers between devices with their start and end apart: 33, of which 23 were waited for; matrix products, arithmetic and copies ran while one was open for 7% of the time, Pallas kernels for 0%

commit v1 on v0

v1 whole, which is shorter than its diff:
```python
import functools

import jax
import jax.numpy as jnp
from jax import lax
from jax.experimental import pallas as pl
from jax.experimental.pallas import tpu as pltpu
from jax.sharding import PartitionSpec as P

time_step = 0.2
viscosity = 0.2
LANES = 128
WINDOWS = 4
SPAN = LANES // WINDOWS
LAG_B, LAG_C, LAG_D = 2, 4, 5


def kernel(pops, tiles, weights, terminal, history, initial, values, density_out,
           gathered, gathered_rim, start_value, start_mass, start_rim,
           rim_send, rim_send_f32, swept, mass_main, slope_r, slope_c, sums_own, sums_all,
           tile_send, tile_recv, tile_self, first_send, first_recv, first_self,
           x_send, x_recv, y_send, y_recv, half_a_send, half_a_recv, half_b_send, half_b_recv,
           core_send, core_recv, back_send, back_recv, back_self):
    steps, rows, cols = history.shape
    width = cols // tiles
    groups = steps // WINDOWS
    total_rows = tiles * rows
    outer = pops // 4
    half = tiles // 2
    me = lax.axis_index("tile")
    own = lax.axis_index("pop")
    core = own % 2
    plane = (own // 2) % 2
    line = own // 4

    def pop_of(a, b, c):
        return (a * 2 + b) * 2 + c

    partner = pop_of(line, plane, 1 - core)
    across = pop_of(line, 1 - plane, core)
    lines = [(line + j) % outer for j in range(1, outer)]
    columns = [pop_of(a, plane, core) for a in lines]
    diagonal = [pop_of(a, 1 - plane, core) for a in lines]
    peers = [(me + d) % tiles for d in range(1, tiles)]

    barrier = pltpu.get_barrier_semaphore()
    greeted = [{"tile": z} for z in peers] + [{"pop": q} for q in [partner, across] + columns]
    for there in greeted:
        pl.semaphore_signal(barrier, inc=1, device_id=there, device_id_type=pl.DeviceIdType.MESH)

    lane = lax.broadcasted_iota(jnp.int32, (rows, LANES), 1)
    window = ((lane + SPAN // 2) % LANES) // SPAN
    right_side = lane < LANES // 2

    def rim_of(block, z):
        right = ((z + 1) % tiles) * width
        left = ((z + tiles - 1) % tiles) * width + width - LANES
        return jnp.where(right_side, block[:, right:right + LANES], block[:, left:left + LANES])

    def packed(parts):
        out = parts[0]
        for k in range(1, len(parts)):
            out = jnp.where(window == k, pltpu.roll(parts[k], SPAN * k, 1), out)
        return out

    for z in range(tiles):
        rim_send_f32[z] = packed([rim_of(terminal[...], z), rim_of(initial[...], z)])
    for g in range(groups):
        for z in range(tiles):
            parts = [rim_of(history[steps - 1 - (g * WINDOWS + k)].astype(jnp.float32), z)
                     for k in range(WINDOWS)]
            rim_send[z, g] = packed(parts).astype(jnp.bfloat16)

    pl.semaphore_wait(barrier, len(greeted))

    def cut(z):
        return pl.ds(pl.multiple_of(z * width, LANES), width)

    sent = []

    def remote(src, dst, send, recv, there):
        copy = pltpu.make_async_remote_copy(src_ref=src, dst_ref=dst, send_sem=send, recv_sem=recv,
                                            device_id=there, device_id_type=pl.DeviceIdType.MESH)
        copy.start()
        return copy

    def arrived(ref, sem):
        pltpu.make_async_copy(ref, ref, sem).wait()

    firsts = [
        (lambda z: terminal.at[:, cut(z)], start_value),
        (lambda z: rim_send_f32.at[z], start_rim),
        (lambda z: initial.at[:, cut(z)], start_mass),
    ]

    def exchange_first(n):
        src, dst = firsts[n]
        pltpu.make_async_copy(src(me), dst.at[me], first_self.at[n]).start()
        for z in peers:
            remote(src(z), dst.at[me], first_send.at[n], first_recv.at[n], {"tile": z})

    def wait_first(n):
        dst = firsts[n][1]
        pltpu.make_async_copy(firsts[n][0](me), dst.at[me], first_self.at[n]).wait()
        arrived(dst.at[pl.ds(0, tiles - 1)], first_recv.at[n])
        arrived(dst.at[pl.ds(0, tiles - 1)], first_send.at[n])

    items = []
    for g in range(groups):
        items.append(("rim", g))
        for k in range(WINDOWS):
            items.append(("main", steps - 1 - (g * WINDOWS + k)))

    def block(n, q):
        kind, index = items[n]
        return gathered.at[q, index] if kind == "main" else gathered_rim.at[q, index]

    def piece(n, z):
        kind, index = items[n]
        return history.at[index, :, cut(z)] if kind == "main" else rim_send.at[z, index]

    def exchange_item(n):
        pltpu.make_async_copy(piece(n, me), block(n, own).at[me], tile_self.at[n]).start()
        for z in peers:
            remote(piece(n, z), block(n, own).at[me], tile_send.at[n], tile_recv.at[n], {"tile": z})

    exchange_item(0)
    exchange_item(1)
    exchange_first(0)
    exchange_first(1)
    for n in range(2, len(items)):
        exchange_item(n)
    exchange_first(2)

    def to_partner(n, kind, q):
        sent.append(remote(block(n, q), block(n, q), core_send.at[kind, n], core_recv.at[kind, n],
                           {"pop": partner}))

    def stage_a(n):
        pltpu.make_async_copy(piece(n, me), block(n, own).at[me], tile_self.at[n]).wait()
        arrived(block(n, own).at[pl.ds(0, tiles - 1)], tile_recv.at[n])
        mine = block(n, own)
        sent.append(remote(mine, mine, x_send.at[n], x_recv.at[n], {"pop": across}))
        for j, q in enumerate(columns):
            sent.append(remote(mine, mine, y_send.at[j, n], y_recv.at[j, n], {"pop": q}))
        to_partner(n, 0, own)

    def part(n, q, which):
        return block(n, q).at[pl.ds(which * half, half)]

    def stage_b(n):
        arrived(block(n, across), x_recv.at[n])
        ref = part(n, across, 1)
        for j, q in enumerate(columns):
            sent.append(remote(ref, ref, half_b_send.at[j, n], half_b_recv.at[j, n], {"pop": q}))
        to_partner(n, 1, across)
        for j in range(outer - 1):
            q = columns[outer - 2 - j]
            arrived(block(n, q), y_recv.at[j, n])
            ref = part(n, q, 0)
            sent.append(remote(ref, ref, half_a_send.at[j, n], half_a_recv.at[j, n], {"pop": across}))
            to_partner(n, 2 + j, q)

    def stage_c(n):
        for j in range(outer - 1):
            q = diagonal[outer - 2 - j]
            arrived(part(n, q, 0), half_a_recv.at[j, n])
            arrived(part(n, q, 1), half_b_recv.at[j, n])
            to_partner(n, 1 + outer + j, q)

    def other(q):
        return q + 1 - 2 * (q % 2)

    def coupled(n):
        for kind in range(2 * outer):
            if kind == 0:
                q = own
            elif kind == 1:
                q = across
            elif kind < 1 + outer:
                q = columns[outer - 2 - (kind - 2)]
            else:
                q = diagonal[outer - 2 - (kind - 1 - outer)]
            arrived(block(n, other(q)), core_recv.at[kind, n])
        total = None
        for q in range(pops):
            factor = weights[own, q].astype(jnp.float32) * (1.0 / pops)
            term = factor * block(n, q)[...].astype(jnp.float32)
            total = term if total is None else total + term
        return total.reshape(total_rows, total.shape[-1])

    full = width + LANES

    def ahead_r(x):
        return pltpu.roll(x, total_rows - 1, 0)

    def behind_r(x):
        return pltpu.roll(x, 1, 0)

    def ahead_c(x):
        return pltpu.roll(x, full - 1, 1)

    def behind_c(x):
        return pltpu.roll(x, 1, 1)

    def rim_at(rim, k):
        return rim if k == 0 else pltpu.roll(rim, LANES - SPAN * k, 1)

    def send_back(src, dst, n):
        pltpu.make_async_copy(src.at[me], dst.at[:, cut(me)], back_self.at[n]).start()
        for z in peers:
            remote(src.at[z], dst.at[:, cut(me)], back_send.at[n], back_recv.at[n], {"tile": z})

    def wait_back(src, dst, n):
        pltpu.make_async_copy(src.at[me], dst.at[:, cut(me)], back_self.at[n]).wait()
        landed = dst.at[:, pl.ds(0, (tiles - 1) * width)]
        arrived(landed, back_recv.at[n])
        arrived(landed, back_send.at[n])

    state = {}

    def stage_d(n):
        kind, t = items[n]
        if n == 0:
            for m in range(2):
                wait_first(m)
            main = start_value[...].reshape(total_rows, width)
            state["u"] = jnp.concatenate([main, start_rim[...].reshape(total_rows, LANES)], axis=1)
        if kind == "rim":
            state["rim"] = coupled(n)
            return
        k = (steps - 1 - t) % WINDOWS
        source = jnp.concatenate([coupled(n), rim_at(state["rim"], k)], axis=1)
        u = state["u"]
        dr = ahead_r(u) - u
        dc = ahead_c(u) - u
        if t + 1 < steps:
            slope_r[t + 1] = dr
            slope_c[t + 1] = dc
        er, ec = behind_r(dr), behind_c(dc)
        br, bc = jnp.maximum(er, 0.0), jnp.maximum(ec, 0.0)
        ar, ac = jnp.minimum(dr, 0.0), jnp.minimum(dc, 0.0)
        lap = (dr - er) + (dc - ec)
        ham = 0.5 * ((br * br + ar * ar) + (bc * bc + ac * ac))
        u = u + time_step * (viscosity * lap - ham + source)
        state["u"] = u
        main = u[:, :width]
        swept[t] = main.reshape(tiles, rows, width)
        send_back(swept.at[t], values.at[t], t)
        line_sum = jnp.sum(main, axis=0, keepdims=True)
        folded = line_sum[:, :LANES]
        for j in range(1, width // LANES):
            folded = folded + line_sum[:, j * LANES:(j + 1) * LANES]
        sums_own[t:t + 1, :] = folded

    count = len(items)
    for i in range(count + LAG_D):
        if i < count:
            stage_a(i)
        if 0 <= i - LAG_B < count:
            stage_b(i - LAG_B)
        if 0 <= i - LAG_C < count:
            stage_c(i - LAG_C)
        if 0 <= i - LAG_D < count:
            stage_d(i - LAG_D)

    sums_n = steps + 1
    sums_all[me] = sums_own[...]
    for z in peers:
        remote(sums_own, sums_all.at[me], back_send.at[sums_n], back_recv.at[sums_n], {"tile": z})

    wait_first(2)
    u = state["u"]
    mass = jnp.concatenate([start_mass[...].reshape(total_rows, width),
                            rim_at(start_rim[...].reshape(total_rows, LANES), 1)], axis=1)
    for t in range(steps):
        if t == 0:
            dr, dc = ahead_r(u) - u, ahead_c(u) - u
        else:
            dr, dc = slope_r[t], slope_c[t]
        mr, mc = ahead_r(mass), ahead_c(mass)
        flux_r = jnp.maximum(-dr, 0.0) * mass + jnp.minimum(-dr, 0.0) * mr
        flux_c = jnp.maximum(-dc, 0.0) * mass + jnp.minimum(-dc, 0.0) * mc
        net_r = viscosity * (mr - mass) - flux_r
        net_c = viscosity * (mc - mass) - flux_c
        mass = mass + time_step * ((net_r - behind_r(net_r)) + (net_c - behind_c(net_c)))
    mass_main[...] = mass[:, :width].reshape(tiles, rows, width)
    send_back(mass_main, density_out, steps)

    arrived(sums_all.at[pl.ds(0, tiles - 1)], back_recv.at[sums_n])
    arrived(sums_all.at[pl.ds(0, tiles - 1)], back_send.at[sums_n])
    grand = jnp.sum(jnp.sum(sums_all[...], axis=0), axis=1, keepdims=True) * (1.0 / (total_rows * cols))
    for t in reversed(range(steps)):
        wait_back(swept.at[t], values.at[t], t)
        values[t] = values[t] - grand[t:t + 1, :]
    wait_back(mass_main, density_out, steps)
    for n in range(count):
        arrived(block(n, own).at[pl.ds(0, tiles - 1)], tile_send.at[n])
    for copy in sent:
        copy.wait_send()


def per_device(pops, tiles, weights, terminal, density_history, density_init):
    _, steps, rows, cols = density_history.shape
    width = cols // tiles
    groups = steps // WINDOWS
    items = steps + groups
    outer = pops // 4
    total_rows = tiles * rows
    full = width + LANES
    dma = pltpu.SemaphoreType.DMA
    lines = max(outer - 1, 1)
    vmem = pl.BlockSpec(memory_space=pltpu.VMEM)
    values, density = pl.pallas_call(
        functools.partial(kernel, pops, tiles),
        out_shape=(
            jax.ShapeDtypeStruct((steps, rows, cols), jnp.float32),
            jax.ShapeDtypeStruct((rows, cols), jnp.float32),
        ),
        in_specs=[pl.BlockSpec(memory_space=pltpu.SMEM), vmem, vmem, vmem],
        out_specs=(vmem, vmem),
        scratch_shapes=[
            pltpu.VMEM((pops, steps, tiles, rows, width), jnp.bfloat16),
            pltpu.VMEM((pops, groups, tiles, rows, LANES), jnp.bfloat16),
            pltpu.VMEM((tiles, rows, width), jnp.float32),
            pltpu.VMEM((tiles, rows, width), jnp.float32),
            pltpu.VMEM((tiles, rows, LANES), jnp.float32),
            pltpu.VMEM((tiles, groups, rows, LANES), jnp.bfloat16),
            pltpu.VMEM((tiles, rows, LANES), jnp.float32),
            pltpu.VMEM((steps, tiles, rows, width), jnp.float32),
            pltpu.VMEM((tiles, rows, width), jnp.float32),
            pltpu.VMEM((steps, total_rows, full), jnp.float32),
            pltpu.VMEM((steps, total_rows, full), jnp.float32),
            pltpu.VMEM((steps, LANES), jnp.float32),
            pltpu.VMEM((tiles, steps, LANES), jnp.float32),
            dma((items,)), dma((items,)), dma((items,)),
            dma((3,)), dma((3,)), dma((3,)),
            dma((items,)), dma((items,)),
            dma((lines, items)), dma((lines, items)),
            dma((lines, items)), dma((lines, items)),
            dma((lines, items)), dma((lines, items)),
            dma((2 * outer, items)), dma((2 * outer, items)),
            dma((steps + 2,)), dma((steps + 2,)), dma((steps + 1,)),
        ],
        compiler_params=pltpu.CompilerParams(collective_id=0, has_side_effects=True),
    )(weights, terminal[0], density_history[0], density_init[0])
    return values[None], density[None]


def solution(mesh):
    in_specs = (P(), P("pop", "tile", None), P("pop", None, "tile", None), P("pop", "tile", None))
    out_specs = (P("pop", None, "tile", None), P("pop", "tile", None))
    body = functools.partial(per_device, mesh.shape["pop"], mesh.shape["tile"])
    return jax.shard_map(body, mesh=mesh, in_specs=in_specs, out_specs=out_specs, check_vma=False)
```

time: 177 us -> 41.7 us (0.24)
  waiting for transfers between devices: 61.8 us -> 0 us
  starting transfers between devices: 52.1 us -> 0 us
  Pallas kernels: 0 us -> 38.4 us
  between operations: 19.6 us -> 0.65 us
  other arithmetic: 16.8 us -> 0 us
  local copies, waits for them, and re-layouts: 13.3 us -> 2.54 us
  blocking collectives: 8.62 us -> 0 us
  matrix products: 4.31 us -> 0 us
    ppermute x32 -> x0, starting transfers between devices: 52.1 us -> none  [the longest x16 30.9 us: padded_2(): after = lax.ppermute(leading, axis, down)]
    pallas_call x0 -> x1, Pallas kernels: none -> 38.4 us  [per_device(): pl.pallas_call(functools.partial(kernel, pops, tiles), out_shape=(jax.Sha...]
    ppermute x32 -> x0, waiting for transfers between devices: 38.2 us -> none  [the longest x16 27.6 us: padded_2(): before = lax.ppermute(last, axis, up)]
    all_gather x1 -> x0, waiting for transfers between devices: 22.9 us -> none  [per_device(): lax.all_gather(density_history, 'pop', axis=0, tiled=True)]
    reduce_sum x8 -> x0, other arithmetic: 12.7 us -> none  [per_device(): local_sums[step] = jnp.sum(advanced)]
    psum x1 -> x0, blocking collectives: 8.62 us -> none  [per_device(): grid_sums = lax.psum(jnp.stack(local_sums), 'tile')]
    slice x51 -> x0, local copies, waits for them, and re-layouts: 8.07 us -> none  [the longest x32 5.71 us: laplace_padded(): jnp.roll(center, -1, 2)]
    another operation x1 -> x0, local copies, waits for them, and re-layouts: 5.17 us -> none  [per_device(): grid_sums = lax.psum(jnp.stack(local_sums), 'tile')]
  transfers between devices with their start and end apart: 33 -> 0, of which waited for: 23 -> 0; matrix products, arithmetic and copies ran while one was open for 7% -> 0% of each run, Pallas kernels for 0% -> 0%
where the time goes in v1:
time: 41.7 us; the launch traced here: 41.6 us
  Pallas kernels  38.4 us (92%)
  local copies, waits for them, and re-layouts  2.54 us (6%)
  between operations  0.65 us (2%)
    pallas_call x1, Pallas kernels, per_device(): pl.pallas_call(functools.partial(kernel, pops, tiles), out_shape=(jax.Sha...  38.4 us
    unnamed x4, local copies, waits for them, and re-layouts  2.54 us

profile of v1, /device:TPU:0, one launch (start us, length us, event | category | flops | bytes accessed | tf_op | source)
XLA Modules:
  0.0 41.6 jit_solution(15048950637814360231)
XLA Ops:
  0.6 38.4 %shard_map.59 = (f32[8,8,2048]{2,1,0:T(8,128)}, f32[8,2048]{1,0:T(8,128)}) custom-call(s32[8,8]{1,0:T(8,128)} %weights.1, f32[8,2048]{1,0:T(8,128)} %bitcast.7, bf16[8,8,2048]{2,1,0:T(8,128)(2,1)} %bitcast.6, f32[8,2048]{1,0:T(8,128)} %bitcast.8), custom_call_target="tpu_custom_call" | custom-call | tf_op jit(solution)/shard_map/pallas_call | solution.py:314
  39.0 0.0 copy-start
  39.0 1.9 %copy.8 = f32[1,8,8,2048]{3,2,1,0:T(8,128)} copy(f32[1,8,8,2048]{3,2,1,0:T(8,128)} %bitcast.5) | data formatting | bytes 1048576
  40.9 0.0 copy-done
  40.9 0.6 %copy.9 = f32[1,8,2048]{2,1,0:T(8,128)} copy(f32[1,8,2048]{2,1,0:T(8,128)S(1)} %bitcast.9) | data formatting | bytes 131072
Async XLA Ops:
  39.0 1.9 %copy-start = (f32[8,2048]{1,0:T(8,128)S(1)}, f32[8,2048]{1,0:T(8,128)}, u32[]{:S(2)}) copy-start(f32[8,2048]{1,0:T(8,128)} %get-tuple-element.5) | copy-start | bytes 196612

commit v2 on v1

--- a/solution.py
+++ b/solution.py
@@ -12,11 +12,12 @@
 LANES = 128
 WINDOWS = 4
 SPAN = LANES // WINDOWS
-LAG_B, LAG_C, LAG_D = 2, 4, 5
-
-
-def kernel(pops, tiles, weights, terminal, history, initial, values, density_out,
-           gathered, gathered_rim, start_value, start_mass, start_rim,
+LAG_B, LAG_C, LAG_D = 3, 3, 4
+DIRECT = 10
+
+
+def kernel(pops, tiles, weights, terminal_in, history_in, initial_in, values, density_out,
+           terminal, history, initial, load_sem, gathered, gathered_rim, start_value, start_mass, start_rim,
            rim_send, rim_send_f32, swept, mass_main, slope_r, slope_c, sums_own, sums_all,
            tile_send, tile_recv, tile_self, first_send, first_recv, first_self,
            x_send, x_recv, y_send, y_recv, half_a_send, half_a_recv, half_b_send, half_b_recv,
@@ -44,10 +45,16 @@
     peers = [(me + d) % tiles for d in range(1, tiles)]
 
     barrier = pltpu.get_barrier_semaphore()
-    greeted = [{"tile": z} for z in peers] + [{"pop": q} for q in [partner, across] + columns]
+    greeted = [{"tile": z} for z in peers] + [{"pop": q} for q in [partner, across] + columns + diagonal]
     for there in greeted:
         pl.semaphore_signal(barrier, inc=1, device_id=there, device_id_type=pl.DeviceIdType.MESH)
 
+    loads = [pltpu.make_async_copy(src, dst, load_sem.at[n]) for n, (src, dst) in enumerate(
+        [(terminal_in, terminal), (initial_in, initial), (history_in, history)])]
+    for load in loads:
+        load.start()
+    for load in loads:
+        load.wait()
     lane = lax.broadcasted_iota(jnp.int32, (rows, LANES), 1)
     window = ((lane + SPAN // 2) % LANES) // SPAN
     right_side = lane < LANES // 2
@@ -136,6 +143,9 @@
         sent.append(remote(block(n, q), block(n, q), core_send.at[kind, n], core_recv.at[kind, n],
                            {"pop": partner}))
 
+    def direct(n):
+        return n >= len(items) - DIRECT
+
     def stage_a(n):
         pltpu.make_async_copy(piece(n, me), block(n, own).at[me], tile_self.at[n]).wait()
         arrived(block(n, own).at[pl.ds(0, tiles - 1)], tile_recv.at[n])
@@ -143,6 +153,9 @@
         sent.append(remote(mine, mine, x_send.at[n], x_recv.at[n], {"pop": across}))
         for j, q in enumerate(columns):
             sent.append(remote(mine, mine, y_send.at[j, n], y_recv.at[j, n], {"pop": q}))
+        if direct(n):
+            for j, q in enumerate(diagonal):
+                sent.append(remote(mine, mine, half_a_send.at[j, n], half_a_recv.at[j, n], {"pop": q}))
         to_partner(n, 0, own)
 
     def part(n, q, which):
@@ -151,21 +164,25 @@
     def stage_b(n):
         arrived(block(n, across), x_recv.at[n])
         ref = part(n, across, 1)
-        for j, q in enumerate(columns):
+        for j, q in enumerate([] if direct(n) else columns):
             sent.append(remote(ref, ref, half_b_send.at[j, n], half_b_recv.at[j, n], {"pop": q}))
         to_partner(n, 1, across)
         for j in range(outer - 1):
             q = columns[outer - 2 - j]
             arrived(block(n, q), y_recv.at[j, n])
             ref = part(n, q, 0)
-            sent.append(remote(ref, ref, half_a_send.at[j, n], half_a_recv.at[j, n], {"pop": across}))
+            if not direct(n):
+                sent.append(remote(ref, ref, half_a_send.at[j, n], half_a_recv.at[j, n], {"pop": across}))
             to_partner(n, 2 + j, q)
 
     def stage_c(n):
         for j in range(outer - 1):
             q = diagonal[outer - 2 - j]
-            arrived(part(n, q, 0), half_a_recv.at[j, n])
-            arrived(part(n, q, 1), half_b_recv.at[j, n])
+            if direct(n):
+                arrived(block(n, q), half_a_recv.at[j, n])
+            else:
+                arrived(part(n, q, 0), half_a_recv.at[j, n])
+                arrived(part(n, q, 1), half_b_recv.at[j, n])
             to_partner(n, 1 + outer + j, q)
 
     def other(q):
@@ -300,6 +317,17 @@
         copy.wait_send()
 
 
+def finish(values, density, values_out, density_out, sems):
+    copies = [
+        pltpu.make_async_copy(values, values_out, sems.at[0]),
+        pltpu.make_async_copy(density, density_out, sems.at[1]),
+    ]
+    for copy in copies:
+        copy.start()
+    for copy in copies:
+        copy.wait()
+
+
 def per_device(pops, tiles, weights, terminal, density_history, density_init):
     _, steps, rows, cols = density_history.shape
     width = cols // tiles
@@ -311,15 +339,20 @@
     dma = pltpu.SemaphoreType.DMA
     lines = max(outer - 1, 1)
     vmem = pl.BlockSpec(memory_space=pltpu.VMEM)
+    anywhere = pl.BlockSpec(memory_space=pl.ANY)
     values, density = pl.pallas_call(
         functools.partial(kernel, pops, tiles),
         out_shape=(
-            jax.ShapeDtypeStruct((steps, rows, cols), jnp.float32),
-            jax.ShapeDtypeStruct((rows, cols), jnp.float32),
+            pltpu.VMEM((steps, rows, cols), jnp.float32),
+            pltpu.VMEM((rows, cols), jnp.float32),
         ),
-        in_specs=[pl.BlockSpec(memory_space=pltpu.SMEM), vmem, vmem, vmem],
+        in_specs=[pl.BlockSpec(memory_space=pltpu.SMEM), anywhere, anywhere, anywhere],
         out_specs=(vmem, vmem),
         scratch_shapes=[
+            pltpu.VMEM((rows, cols), jnp.float32),
+            pltpu.VMEM((steps, rows, cols), jnp.bfloat16),
+            pltpu.VMEM((rows, cols), jnp.float32),
+            dma((3,)),
             pltpu.VMEM((pops, steps, tiles, rows, width), jnp.bfloat16),
             pltpu.VMEM((pops, groups, tiles, rows, LANES), jnp.bfloat16),
             pltpu.VMEM((tiles, rows, width), jnp.float32),
@@ -344,6 +377,17 @@
         ],
         compiler_params=pltpu.CompilerParams(collective_id=0, has_side_effects=True),
     )(weights, terminal[0], density_history[0], density_init[0])
+    values, density = pl.pallas_call(
+        finish,
+        out_shape=(
+            jax.ShapeDtypeStruct((steps, rows, cols), jnp.float32),
+            jax.ShapeDtypeStruct((rows, cols), jnp.float32),
+        ),
+        in_specs=[anywhere, anywhere],
+        out_specs=(anywhere, anywhere),
+        scratch_shapes=[dma((2,))],
+        compiler_params=pltpu.CompilerParams(vmem_limit_bytes=8 * 1024 * 1024),
+    )(values, density)
     return values[None], density[None]
 
 

time: 41.7 us -> 36.8 us (0.88)
  local copies, waits for them, and re-layouts: 2.54 us -> 0 us
  Pallas kernels: 38.4 us -> 35.9 us
    unnamed x4 -> x0, local copies, waits for them, and re-layouts: 2.54 us -> none
    pallas_call x1 -> x2, Pallas kernels: 38.4 us -> 35.9 us  [the longest x1 35.1 us: per_device(): pl.pallas_call(functools.partial(kernel, pops, tiles), out_shape=(pltpu.V...]
where the time goes in v2:
time: 36.8 us; the launch traced here: 36.6 us
  Pallas kernels  35.9 us (98%)
  between operations  0.64 us (2%)
    pallas_call x1, Pallas kernels, per_device(): pl.pallas_call(functools.partial(kernel, pops, tiles), out_shape=(pltpu.V...  35.1 us
    pallas_call x1, Pallas kernels, per_device(): pl.pallas_call(finish, out_shape=(jax.ShapeDtypeStruct((steps, rows, cols...  0.82 us

profile of v2, /device:TPU:0, one launch (start us, length us, event | category | flops | bytes accessed | tf_op | source)
XLA Modules:
  0.0 36.6 jit_solution(947265643889522673)
XLA Ops:
  0.6 35.1 %shard_map.59 = (f32[8,8,2048]{2,1,0:T(8,128)S(1)}, f32[8,2048]{1,0:T(8,128)S(1)}) custom-call(s32[8,8]{1,0:T(8,128)} %weights.1, f32[8,2048]{1,0:T(8,128)} %bitcast.6, bf16[8,8,2048]{2,1,0:T(8,128)(2,1)} %bitcast.5, f32[8,2048]{1,0:T(8,128)} %bitcast.7), custom_call_target="tpu_custom_call" | custom-call | tf_op jit(solution)/shard_map/pallas_call | solution.py:343
  35.8 0.8 %shard_map.60 = (f32[8,8,2048]{2,1,0:T(8,128)}, f32[8,2048]{1,0:T(8,128)}) custom-call(f32[8,8,2048]{2,1,0:T(8,128)S(1)} %get-tuple-element.6.values, f32[8,2048]{1,0:T(8,128)S(1)} %get-tuple-element.7.density), custom_call_target="tpu_custom_call" | custom-call | tf_op jit(solution)/shard_map/pallas_call | solution.py:380

commit v3 on v2

--- a/solution.py
+++ b/solution.py
@@ -14,6 +14,7 @@
 SPAN = LANES // WINDOWS
 LAG_B, LAG_C, LAG_D = 3, 3, 4
 DIRECT = 10
+TWIN = 1
 
 
 def kernel(pops, tiles, weights, terminal_in, history_in, initial_in, values, density_out,
@@ -45,7 +46,9 @@
     peers = [(me + d) % tiles for d in range(1, tiles)]
 
     barrier = pltpu.get_barrier_semaphore()
-    greeted = [{"tile": z} for z in peers] + [{"pop": q} for q in [partner, across] + columns + diagonal]
+    far = [across] + columns + diagonal
+    far_twin = [q + 1 - 2 * (q % 2) for q in far]
+    greeted = [{"tile": z} for z in peers] + [{"pop": q} for q in [partner] + far + far_twin]
     for there in greeted:
         pl.semaphore_signal(barrier, inc=1, device_id=there, device_id_type=pl.DeviceIdType.MESH)
 
@@ -145,6 +148,12 @@
 
     def direct(n):
         return n >= len(items) - DIRECT
+
+    def twin(n):
+        return n >= len(items) - TWIN
+
+    def twin_slot(kind):
+        return kind
 
     def stage_a(n):
         pltpu.make_async_copy(piece(n, me), block(n, own).at[me], tile_self.at[n]).wait()
@@ -156,6 +165,9 @@
         if direct(n):
             for j, q in enumerate(diagonal):
                 sent.append(remote(mine, mine, half_a_send.at[j, n], half_a_recv.at[j, n], {"pop": q}))
+        if twin(n):
+            for kind, q in enumerate(far_twin):
+                sent.append(remote(mine, mine, core_send.at[kind + 1, n], core_recv.at[twin_slot(kind + 1), n], {"pop": q}))
         to_partner(n, 0, own)
 
     def part(n, q, which):
@@ -166,14 +178,16 @@
         ref = part(n, across, 1)
         for j, q in enumerate([] if direct(n) else columns):
             sent.append(remote(ref, ref, half_b_send.at[j, n], half_b_recv.at[j, n], {"pop": q}))
-        to_partner(n, 1, across)
+        if not twin(n):
+            to_partner(n, 1, across)
         for j in range(outer - 1):
             q = columns[outer - 2 - j]
             arrived(block(n, q), y_recv.at[j, n])
             ref = part(n, q, 0)
             if not direct(n):
                 sent.append(remote(ref, ref, half_a_send.at[j, n], half_a_recv.at[j, n], {"pop": across}))
-            to_partner(n, 2 + j, q)
+            if not twin(n):
+                to_partner(n, 2 + j, q)
 
     def stage_c(n):
         for j in range(outer - 1):
@@ -183,7 +197,8 @@
             else:
                 arrived(part(n, q, 0), half_a_recv.at[j, n])
                 arrived(part(n, q, 1), half_b_recv.at[j, n])
-            to_partner(n, 1 + outer + j, q)
+            if not twin(n):
+                to_partner(n, 1 + outer + j, q)
 
     def other(q):
         return q + 1 - 2 * (q % 2)

time: 36.8 us -> 36.8 us (level)
  no operation moved by 1% of the time
where the time goes in v3:
time: 36.8 us; the launch traced here: 36.6 us
  Pallas kernels  35.9 us (98%)
  between operations  0.64 us (2%)
    pallas_call x1, Pallas kernels, per_device(): pl.pallas_call(functools.partial(kernel, pops, tiles), out_shape=(pltpu.V...  35.1 us
    pallas_call x1, Pallas kernels, per_device(): pl.pallas_call(finish, out_shape=(jax.ShapeDtypeStruct((steps, rows, cols...  0.82 us

profile of v3, /device:TPU:0, one launch (start us, length us, event | category | flops | bytes accessed | tf_op | source)
XLA Modules:
  0.0 36.6 jit_solution(1768932240251117362)
XLA Ops:
  0.6 35.1 %shard_map.59 = (f32[8,8,2048]{2,1,0:T(8,128)S(1)}, f32[8,2048]{1,0:T(8,128)S(1)}) custom-call(s32[8,8]{1,0:T(8,128)} %weights.1, f32[8,2048]{1,0:T(8,128)} %bitcast.6, bf16[8,8,2048]{2,1,0:T(8,128)(2,1)} %bitcast.5, f32[8,2048]{1,0:T(8,128)} %bitcast.7), custom_call_target="tpu_custom_call" | custom-call | tf_op jit(solution)/shard_map/pallas_call | solution.py:358
  35.8 0.8 %shard_map.60 = (f32[8,8,2048]{2,1,0:T(8,128)}, f32[8,2048]{1,0:T(8,128)}) custom-call(f32[8,8,2048]{2,1,0:T(8,128)S(1)} %get-tuple-element.6.values, f32[8,2048]{1,0:T(8,128)S(1)} %get-tuple-element.7.density), custom_call_target="tpu_custom_call" | custom-call | tf_op jit(solution)/shard_map/pallas_call | solution.py:395
